TPU v7x, 32 devices: a whole 2x2x4 slice. The times are simulated.
32 devices in a mesh: seq: 32 (over z, y, x, core).
Axes of the slice: x: 2, y: 2, z: 4, core: 2. Of those that a mesh axis runs over, the one named last changes fastest.
Arguments:
- values: bfloat16 [16384, 2048], P('seq'), may hold values from -6 to 6
- keys_queries: bfloat16 [16384, 128], P('seq'), may hold values from -2 to 2
- step_size: float32 [16384, 32], P('seq'), may hold values from 0.1 to 1.9
- level_logits: float32 [16384, 480], P('seq'), may hold values from -6 to 6
- decay_rate: float32 [32], replicated, may hold values from 1.2207031e-05 to 0.03
- resets: int32 [32], P('seq'), may hold values 0 or 1
Outputs:
- mixed: bfloat16 [16384, 2048], P('seq')
Inputs may be any that keep to these rules, and one draw needn't show every extreme that they name: resets[b] is 1 where a document starts at the first token of block b.
All inputs are finite; a program needn't handle non-finite values.
Results may differ from a plain program's by a relative error of at most 0.0012.
The roundings to bfloat16 on the way count: a program that leaves them out, or rounds other values in their place, can miss the bound.
Values sent between devices are 32-bit elements; how exact they have to be, the bound alone decides.
A program may use at most 64 MiB of HBM per device.

v0:
```python
import jax
import jax.numpy as jnp
from jax import lax
from jax.sharding import PartitionSpec as P


def partner_2(block, axis, bit):
    count = lax.axis_size(axis)
    route = []
    for low in range(count):
        high = low | 1 << bit
        if high != low and high < count:
            route += [(low, high), (high, low)]
    return lax.ppermute(block, axis, route)


def level_table(length, inner_levels):
    position = jnp.arange(length, dtype=jnp.int32)
    differ = position[:, None] ^ position[None, :]
    level_map = jnp.zeros((length, length), jnp.int32)
    for power_no in range(inner_levels - 1):
        level_map = level_map + (differ >= 1 << power_no).astype(jnp.int32)
    causal = position[:, None] >= position[None, :]
    return (level_map, causal)


def local(values, keys_queries, step_size, level_logits, decay_rate, resets):
    length = values.shape[0]
    head_count = decay_rate.shape[0]
    head_dim = values.shape[1] // head_count
    state_dim = keys_queries.shape[1] // 2
    inner_levels = length.bit_length()
    block_count = lax.axis_size("seq")
    outer_levels = block_count.bit_length() - 1
    own_index = lax.axis_index("seq")
    level_map, causal = level_table(length, inner_levels)
    block_values = values.reshape(length, head_count, head_dim)
    key_rows = keys_queries[:, :state_dim]
    queries = keys_queries[:, state_dim:]
    decay_sum = jnp.cumsum(-step_size * decay_rate[None, :], axis=0)
    weights = jax.nn.softplus(level_logits).reshape(length, inner_levels + outer_levels, head_count)
    to_end = jnp.exp(decay_sum[-1][None, :] - decay_sum)
    decayed = (key_rows.astype(jnp.float32).T[None] * to_end.T[:, None, :]).astype(jnp.bfloat16)
    range_state = jnp.einsum(
        "hnl,lhp->hnp", decayed, block_values, preferred_element_type=jnp.float32
    )
    entering = 1.0 - resets.astype(jnp.float32)[0]
    block_total = entering * jnp.exp(decay_sum[-1])
    prefix_decay = jnp.ones((head_count,), jnp.float32)
    range_total = block_total
    levels = []
    for bit_no in range(outer_levels):
        in_upper = own_index // (1 << bit_no) % 2 == 1
        partner, partner_total = partner_2((range_state, range_total), "seq", bit_no)
        levels.append(jnp.where(in_upper, partner * (prefix_decay * entering)[:, None, None], 0.0))
        range_state = jnp.where(
            in_upper,
            range_state + range_total[:, None, None] * partner,
            partner + partner_total[:, None, None] * range_state,
        )
        prefix_decay = jnp.where(in_upper, prefix_decay * partner_total, prefix_decay)
        range_total = range_total * partner_total
    states = (
        jnp.stack(levels, 1)
        .astype(jnp.bfloat16)
        .reshape(head_count, outer_levels * state_dim, head_dim)
    )
    scores = jnp.dot(queries, key_rows.T, preferred_element_type=jnp.float32)
    group_size = 4
    group_count = head_count // group_size
    sum_grouped = decay_sum.T.reshape(group_count, group_size, length)
    weight_grouped = weights.transpose(2, 1, 0).reshape(
        group_count, group_size, inner_levels + outer_levels, length
    )
    values_grouped = block_values.reshape(length, group_count, group_size, head_dim).transpose(
        1, 0, 2, 3
    )
    states_grouped = states.reshape(group_count, group_size, outer_levels * state_dim, head_dim)
    query_wide = queries.astype(jnp.float32)

    def group_output(packed):
        group_sum, group_weight, group_values, group_states = packed
        log_gap = group_sum[:, :, None] - group_sum[:, None, :]
        decays = jnp.exp(jnp.where(causal[None], log_gap, -1e30))
        level_mix = jnp.zeros((group_size, length, length), jnp.float32)
        for level_no in range(inner_levels):
            level_mix = level_mix + jnp.where(
                level_map[None] == level_no, group_weight[:, level_no, :, None], 0.0
            )
        mixing = (scores[None] * decays * level_mix).astype(jnp.bfloat16)
        local_term = jnp.einsum(
            "gts,sgp->tgp", mixing, group_values, preferred_element_type=jnp.float32
        )
        scaled = jnp.exp(group_sum)[:, None, :] * group_weight[:, inner_levels:, :]
        read_rows = (scaled[:, :, :, None] * query_wide[None, None]).astype(jnp.bfloat16)
        read_rows = read_rows.transpose(0, 2, 1, 3).reshape(
            group_size, length, outer_levels * state_dim
        )
        cross_term = jnp.einsum(
            "gtk,gkp->tgp", read_rows, group_states, preferred_element_type=jnp.float32
        )
        return local_term + cross_term

    outputs = lax.map(group_output, (sum_grouped, weight_grouped, values_grouped, states_grouped))
    return outputs.transpose(1, 0, 2, 3).reshape(length, head_count * head_dim).astype(jnp.bfloat16)


def solution(mesh):
    placed = (P("seq", None), P("seq", None), P("seq", None), P("seq", None), P(), P("seq"))
    return jax.shard_map(
        local, mesh=mesh, in_specs=placed, out_specs=P("seq", None), check_vma=False
    )
```

profile of v0, /device:TPU:0, one launch (start us, length us, event | category | flops | bytes accessed | tf_op | source)
XLA Modules:
  0.0 250.1 jit_solution(15290697751392461681)
XLA Ops:
  0.0 0.9 copy_bitcast_fusion
  1.0 1.1 reduce-window.6
  2.7 3.9 %copy.37 = bf16[512,2048]{0,1:T(8,128)(2,1)} copy(bf16[512,2048]{1,0:T(8,128)(2,1)} %param.8) | data formatting | bytes 4194304 | tf_op args[0]
  6.9 2.3 fusion.43
  10.5 1.5 collective-permute-done.1
  12.3 2.9 %collective-permute-start.2 = (f32[32,64,64]{2,1,0:T(8,128)S(1)}, f32[32,64,64]{2,1,0:T(8,128)S(1)}, u32[]{:S(2)}, u32[]{:S(2)}) collective-permute-start(f32[32,64,64]{2,1,0:T(8,128)S(1)} %add_select_fusion.3), channel_id=1, source_target_pairs={{0,2},{2,0},{1,3},{3,1},{4,6},{6,4},{5,7},{7,5},{8,10},{10,8},{9,1... | collective-permute-start | bytes 1572872 | tf_op jit(solution)/shard_map/ppermute | solution.py:14
  15.2 1.3 fusion.56
  16.5 2.7 %compare_select_fusion = f32[512,480]{0,1:T(8,128)} fusion(f32[512,480]{0,1:T(8,128)} %param.11), kind=kLoop, calls=%fused_computation.65 | loop fusion | flops 1474560 | bytes 1966080 | tf_op jit(solution)/shard_map/jit(softplus)/select_n | solution.py:41
  19.2 19.5 %collective-permute-done.3 = f32[32]{0:T(128)S(1)} collective-permute-done((f32[32]{0:T(128)S(1)}, f32[32]{0:T(128)S(1)}, u32[]{:S(2)}, u32[]{:S(2)}) %collective-permute-start.3) | collective-permute-done | bytes 160 | tf_op jit(solution)/shard_map/ppermute | solution.py:14
  38.7 1.3 add_select_fusion.2
  40.0 1.8 collective-permute-start.4
  42.5 22.3 %collective-permute-done.5 = f32[32]{0:T(128)S(1)} collective-permute-done((f32[32]{0:T(128)S(1)}, f32[32]{0:T(128)S(1)}, u32[]{:S(2)}, u32[]{:S(2)}) %collective-permute-start.5) | collective-permute-done | bytes 160 | tf_op jit(solution)/shard_map/ppermute | solution.py:14
  64.9 1.6 collective-permute-start.7
  66.4 2.5 reshape.118
  68.9 1.8 add_select_fusion.1
  70.7 1.2 collective-permute-start.6
  72.3 21.6 %collective-permute-done.6 = f32[32,64,64]{2,1,0:T(8,128)S(1)} collective-permute-done((f32[32,64,64]{2,1,0:T(8,128)S(1)}, f32[32,64,64]{2,1,0:T(8,128)S(1)}, u32[]{:S(2)}, u32[]{:S(2)}) %collective-permute-start.6) | collective-permute-done | bytes 524320 | tf_op jit(solution)/shard_map/ppermute | solution.py:14
  94.2 3.8 %collective-permute-start.8 = (f32[32,64,64]{2,1,0:T(8,128)S(1)}, f32[32,64,64]{2,1,0:T(8,128)S(1)}, u32[]{:S(2)}, u32[]{:S(2)}) collective-permute-start(f32[32,64,64]{2,1,0:T(8,128)S(1)} %add_select_fusion), channel_id=1, source_target_pairs={{0,16},{16,0},{1,17},{17,1},{2,18},{18,2},{3,19},{19,3},{4,20},{20... | collective-permute-start | bytes 1572872 | tf_op jit(solution)/shard_map/ppermute | solution.py:14
  98.0 1.5 fusion.51
  99.7 40.1 %collective-permute-done.8 = f32[32,64,64]{2,1,0:T(8,128)S(1)} collective-permute-done((f32[32,64,64]{2,1,0:T(8,128)S(1)}, f32[32,64,64]{2,1,0:T(8,128)S(1)}, u32[]{:S(2)}, u32[]{:S(2)}) %collective-permute-start.8) | collective-permute-done | bytes 524320 | tf_op jit(solution)/shard_map/ppermute | solution.py:14
  140.0 0.6 copy.44
  140.6 2.8 %copy.46 = bf16[8,4,320,64]{2,3,1,0:T(8,128)(2,1)} copy(bf16[8,4,320,64]{3,2,1,0:T(8,128)(2,1)S(1)} %bitcast.120) | data formatting | bytes 2621440
  143.4 102.8 %while.12 = (s32[]{:T(128)}, bf16[8,512,4,64]{1,3,2,0:T(8,128)(2,1)}, bf16[8,512,4,64]{1,3,2,0:T(8,128)(2,1)}, f32[512,512]{1,0:T(8,128)}, f32[8,4,512]{2,1,0:T(...) while((s32[]{:T(128)}, ...), condition=%wide.region_3.4_spmd.clone.clone, body=%wide.region_2.3_spmd.clone.clone.sunk | while | flops 290072576 | bytes 17852032 | solution.py:104
  143.4 1.0 dynamic-slice_bitcast_fusion.4
  146.4 7.4 %fusion.87 = f32[4,64,512]{2,1,0:T(8,128)S(1)} fusion(f32[4,512]{1,0:T(4,128)S(1)} %get-tuple-element.268, f32[4,512]{1,0:T(4,128)S(1)} %get-tuple-element.269, f32[4,512]{1,0:T(4,128)S(1)} %get-tuple-element.270, f32[4,512]{1,0:T(4,128)S(1)} %get-tuple-element.271, f32[4,512]{1,0:T(4,128)S(1)} %get-tuple-element.272, ...), kind=kOutput, calls=%fused_computation.5.clone.1 | convolution fusion | flops 159383552 | bytes 4817408 | tf_op jit(solution)/shard_map/while/body/eval_jaxpr/gts,sgp->tgp/dot_general | solution.py:91
  154.2 2.0 fusion.90
  156.2 1.0 dynamic-slice_bitcast_fusion.4
  159.2 7.4 %fusion.87 = f32[4,64,512]{2,1,0:T(8,128)S(1)} fusion(f32[4,512]{1,0:T(4,128)S(1)} %get-tuple-element.268, f32[4,512]{1,0:T(4,128)S(1)} %get-tuple-element.269, f32[4,512]{1,0:T(4,128)S(1)} %get-tuple-element.270, f32[4,512]{1,0:T(4,128)S(1)} %get-tuple-element.271, f32[4,512]{1,0:T(4,128)S(1)} %get-tuple-element.272, ...), kind=kOutput, calls=%fused_computation.5.clone.1 | convolution fusion | flops 159383552 | bytes 4817408 | tf_op jit(solution)/shard_map/while/body/eval_jaxpr/gts,sgp->tgp/dot_general | solution.py:91
  167.1 2.0 fusion.90
  169.1 1.0 dynamic-slice_bitcast_fusion.4
  172.1 7.4 %fusion.87 = f32[4,64,512]{2,1,0:T(8,128)S(1)} fusion(f32[4,512]{1,0:T(4,128)S(1)} %get-tuple-element.268, f32[4,512]{1,0:T(4,128)S(1)} %get-tuple-element.269, f32[4,512]{1,0:T(4,128)S(1)} %get-tuple-element.270, f32[4,512]{1,0:T(4,128)S(1)} %get-tuple-element.271, f32[4,512]{1,0:T(4,128)S(1)} %get-tuple-element.272, ...), kind=kOutput, calls=%fused_computation.5.clone.1 | convolution fusion | flops 159383552 | bytes 4817408 | tf_op jit(solution)/shard_map/while/body/eval_jaxpr/gts,sgp->tgp/dot_general | solution.py:91
  179.9 2.0 fusion.90
  181.9 1.0 dynamic-slice_bitcast_fusion.4
  184.9 7.4 %fusion.87 = f32[4,64,512]{2,1,0:T(8,128)S(1)} fusion(f32[4,512]{1,0:T(4,128)S(1)} %get-tuple-element.268, f32[4,512]{1,0:T(4,128)S(1)} %get-tuple-element.269, f32[4,512]{1,0:T(4,128)S(1)} %get-tuple-element.270, f32[4,512]{1,0:T(4,128)S(1)} %get-tuple-element.271, f32[4,512]{1,0:T(4,128)S(1)} %get-tuple-element.272, ...), kind=kOutput, calls=%fused_computation.5.clone.1 | convolution fusion | flops 159383552 | bytes 4817408 | tf_op jit(solution)/shard_map/while/body/eval_jaxpr/gts,sgp->tgp/dot_general | solution.py:91
  192.7 2.0 fusion.90
  194.8 1.0 dynamic-slice_bitcast_fusion.4
  197.8 7.4 %fusion.87 = f32[4,64,512]{2,1,0:T(8,128)S(1)} fusion(f32[4,512]{1,0:T(4,128)S(1)} %get-tuple-element.268, f32[4,512]{1,0:T(4,128)S(1)} %get-tuple-element.269, f32[4,512]{1,0:T(4,128)S(1)} %get-tuple-element.270, f32[4,512]{1,0:T(4,128)S(1)} %get-tuple-element.271, f32[4,512]{1,0:T(4,128)S(1)} %get-tuple-element.272, ...), kind=kOutput, calls=%fused_computation.5.clone.1 | convolution fusion | flops 159383552 | bytes 4817408 | tf_op jit(solution)/shard_map/while/body/eval_jaxpr/gts,sgp->tgp/dot_general | solution.py:91
  205.6 2.0 fusion.90
  207.6 1.0 dynamic-slice_bitcast_fusion.4
  210.6 7.4 %fusion.87 = f32[4,64,512]{2,1,0:T(8,128)S(1)} fusion(f32[4,512]{1,0:T(4,128)S(1)} %get-tuple-element.268, f32[4,512]{1,0:T(4,128)S(1)} %get-tuple-element.269, f32[4,512]{1,0:T(4,128)S(1)} %get-tuple-element.270, f32[4,512]{1,0:T(4,128)S(1)} %get-tuple-element.271, f32[4,512]{1,0:T(4,128)S(1)} %get-tuple-element.272, ...), kind=kOutput, calls=%fused_computation.5.clone.1 | convolution fusion | flops 159383552 | bytes 4817408 | tf_op jit(solution)/shard_map/while/body/eval_jaxpr/gts,sgp->tgp/dot_general | solution.py:91
  218.4 2.0 fusion.90
  220.5 1.0 dynamic-slice_bitcast_fusion.4
  223.5 7.4 %fusion.87 = f32[4,64,512]{2,1,0:T(8,128)S(1)} fusion(f32[4,512]{1,0:T(4,128)S(1)} %get-tuple-element.268, f32[4,512]{1,0:T(4,128)S(1)} %get-tuple-element.269, f32[4,512]{1,0:T(4,128)S(1)} %get-tuple-element.270, f32[4,512]{1,0:T(4,128)S(1)} %get-tuple-element.271, f32[4,512]{1,0:T(4,128)S(1)} %get-tuple-element.272, ...), kind=kOutput, calls=%fused_computation.5.clone.1 | convolution fusion | flops 159383552 | bytes 4817408 | tf_op jit(solution)/shard_map/while/body/eval_jaxpr/gts,sgp->tgp/dot_general | solution.py:91
  231.3 2.0 fusion.90
  233.3 1.0 dynamic-slice_bitcast_fusion.4
  236.3 7.4 %fusion.87 = f32[4,64,512]{2,1,0:T(8,128)S(1)} fusion(f32[4,512]{1,0:T(4,128)S(1)} %get-tuple-element.268, f32[4,512]{1,0:T(4,128)S(1)} %get-tuple-element.269, f32[4,512]{1,0:T(4,128)S(1)} %get-tuple-element.270, f32[4,512]{1,0:T(4,128)S(1)} %get-tuple-element.271, f32[4,512]{1,0:T(4,128)S(1)} %get-tuple-element.272, ...), kind=kOutput, calls=%fused_computation.5.clone.1 | convolution fusion | flops 159383552 | bytes 4817408 | tf_op jit(solution)/shard_map/while/body/eval_jaxpr/gts,sgp->tgp/dot_general | solution.py:91
  244.1 2.0 fusion.90
  246.2 3.9 %copy.47 = bf16[512,2048]{1,0:T(8,128)(2,1)} copy(bf16[512,2048]{0,1:T(8,128)(2,1)} %bitcast.122) | data formatting | bytes 4194304 | tf_op jit(solution)/shard_map/convert_element_type | solution.py:105
  (148 shorter events, 21.8 us)
Async XLA Ops:
  0.0 6.6 %copy-start = (bf16[512,128]{1,0:T(8,128)(2,1)S(1)}, bf16[512,128]{1,0:T(8,128)(2,1)}, u32[]{:S(2)}) copy-start(bf16[512,128]{1,0:T(8,128)(2,1)} %param.9) | copy-start | bytes 393220
  9.2 2.8 %collective-permute-start = (f32[32,64,64]{2,1,0:T(8,128)S(1)}, f32[32,64,64]{2,1,0:T(8,128)S(1)}, u32[]{:S(2)}, u32[]{:S(2)}) collective-permute-start(f32[32,64,64]{2,1,0:T(8,128)S(1)} %fusion.43), channel_id=1, source_target_pairs={{0,1},{1,0},{2,3},{3,2},{4,5},{5,4},{6,7},{7,6},{8,9},{9,8},{10,11... | collective-permute-start | bytes 1572872 | tf_op jit(solution)/shard_map/ppermute | solution.py:14
  10.4 1.6 collective-permute-start.1
  12.3 26.5 %collective-permute-start.2 = (f32[32,64,64]{2,1,0:T(8,128)S(1)}, f32[32,64,64]{2,1,0:T(8,128)S(1)}, u32[]{:S(2)}, u32[]{:S(2)}) collective-permute-start(f32[32,64,64]{2,1,0:T(8,128)S(1)} %add_select_fusion.3), channel_id=1, source_target_pairs={{0,2},{2,0},{1,3},{3,1},{4,6},{6,4},{5,7},{7,5},{8,10},{10,8},{9,1... | collective-permute-start | bytes 1572872 | tf_op jit(solution)/shard_map/ppermute | solution.py:14
  19.2 19.5 %collective-permute-start.3 = (f32[32]{0:T(128)S(1)}, f32[32]{0:T(128)S(1)}, u32[]{:S(2)}, u32[]{:S(2)}) collective-permute-start(f32[32]{0:T(128)S(1)} %fusion.65), channel_id=1, source_target_pairs={{0,2},{2,0},{1,3},{3,1},{4,6},{6,4},{5,7},{7,5},{8,10},{10,8},{9,1... | collective-permute-start | bytes 392 | tf_op jit(solution)/shard_map/ppermute | solution.py:14
  40.0 28.9 %collective-permute-start.4 = (f32[32,64,64]{2,1,0:T(8,128)}, f32[32,64,64]{2,1,0:T(8,128)}, u32[]{:S(2)}, u32[]{:S(2)}) collective-permute-start(f32[32,64,64]{2,1,0:T(8,128)} %add_select_fusion.2), channel_id=1, source_target_pairs={{0,4},{4,0},{1,5},{5,1},{2,6},{6,2},{3,7},{7,3},{8,12},{12,8},{9,1... | collective-permute-start | bytes 1572872 | tf_op jit(solution)/shard_map/ppermute | solution.py:14
  42.1 22.8 %collective-permute-start.5 = (f32[32]{0:T(128)S(1)}, f32[32]{0:T(128)S(1)}, u32[]{:S(2)}, u32[]{:S(2)}) collective-permute-start(f32[32]{0:T(128)S(1)} %mul.237), channel_id=1, source_target_pairs={{0,4},{4,0},{1,5},{5,1},{2,6},{6,2},{3,7},{7,3},{8,12},{12,8},{9,1... | collective-permute-start | bytes 392 | tf_op jit(solution)/shard_map/ppermute | solution.py:14
  64.9 4.0 %collective-permute-start.7 = (f32[32]{0:T(128)S(1)}, f32[32]{0:T(128)S(1)}, u32[]{:S(2)}, u32[]{:S(2)}) collective-permute-start(f32[32]{0:T(128)S(1)} %mul.246), channel_id=1, source_target_pairs={{0,8},{8,0},{1,9},{9,1},{2,10},{10,2},{3,11},{11,3},{4,12},{12,4},... | collective-permute-start | bytes 392 | tf_op jit(solution)/shard_map/ppermute | solution.py:14
  70.7 23.2 %collective-permute-start.6 = (f32[32,64,64]{2,1,0:T(8,128)S(1)}, f32[32,64,64]{2,1,0:T(8,128)S(1)}, u32[]{:S(2)}, u32[]{:S(2)}) collective-permute-start(f32[32,64,64]{2,1,0:T(8,128)S(1)} %add_select_fusion.1), channel_id=1, source_target_pairs={{0,8},{8,0},{1,9},{9,1},{2,10},{10,2},{3,11},{11,3},{4,12},{12,4},... | collective-permute-start | bytes 1572872 | tf_op jit(solution)/shard_map/ppermute | solution.py:14
  94.2 45.6 %collective-permute-start.8 = (f32[32,64,64]{2,1,0:T(8,128)S(1)}, f32[32,64,64]{2,1,0:T(8,128)S(1)}, u32[]{:S(2)}, u32[]{:S(2)}) collective-permute-start(f32[32,64,64]{2,1,0:T(8,128)S(1)} %add_select_fusion), channel_id=1, source_target_pairs={{0,16},{16,0},{1,17},{17,1},{2,18},{18,2},{3,19},{19,3},{4,20},{20... | collective-permute-start | bytes 1572872 | tf_op jit(solution)/shard_map/ppermute | solution.py:14
  143.4 3.0 %copy-start.1 = (f32[512,512]{1,0:T(8,128)S(1)}, f32[512,512]{1,0:T(8,128)}, u32[]{:S(2)}) copy-start(f32[512,512]{1,0:T(8,128)} %get-tuple-element.311) | copy-start | bytes 3145732 | tf_op jit(solution)/shard_map/while
  156.2 3.0 %copy-start.1 = (f32[512,512]{1,0:T(8,128)S(1)}, f32[512,512]{1,0:T(8,128)}, u32[]{:S(2)}) copy-start(f32[512,512]{1,0:T(8,128)} %get-tuple-element.311) | copy-start | bytes 3145732 | tf_op jit(solution)/shard_map/while
  169.1 3.0 %copy-start.1 = (f32[512,512]{1,0:T(8,128)S(1)}, f32[512,512]{1,0:T(8,128)}, u32[]{:S(2)}) copy-start(f32[512,512]{1,0:T(8,128)} %get-tuple-element.311) | copy-start | bytes 3145732 | tf_op jit(solution)/shard_map/while
  181.9 3.0 %copy-start.1 = (f32[512,512]{1,0:T(8,128)S(1)}, f32[512,512]{1,0:T(8,128)}, u32[]{:S(2)}) copy-start(f32[512,512]{1,0:T(8,128)} %get-tuple-element.311) | copy-start | bytes 3145732 | tf_op jit(solution)/shard_map/while
  194.8 3.0 %copy-start.1 = (f32[512,512]{1,0:T(8,128)S(1)}, f32[512,512]{1,0:T(8,128)}, u32[]{:S(2)}) copy-start(f32[512,512]{1,0:T(8,128)} %get-tuple-element.311) | copy-start | bytes 3145732 | tf_op jit(solution)/shard_map/while
  207.6 3.0 %copy-start.1 = (f32[512,512]{1,0:T(8,128)S(1)}, f32[512,512]{1,0:T(8,128)}, u32[]{:S(2)}) copy-start(f32[512,512]{1,0:T(8,128)} %get-tuple-element.311) | copy-start | bytes 3145732 | tf_op jit(solution)/shard_map/while
  220.4 3.0 %copy-start.1 = (f32[512,512]{1,0:T(8,128)S(1)}, f32[512,512]{1,0:T(8,128)}, u32[]{:S(2)}) copy-start(f32[512,512]{1,0:T(8,128)} %get-tuple-element.311) | copy-start | bytes 3145732 | tf_op jit(solution)/shard_map/while
  233.3 3.0 %copy-start.1 = (f32[512,512]{1,0:T(8,128)S(1)}, f32[512,512]{1,0:T(8,128)}, u32[]{:S(2)}) copy-start(f32[512,512]{1,0:T(8,128)} %get-tuple-element.311) | copy-start | bytes 3145732 | tf_op jit(solution)/shard_map/while
where the time goes:
time: 251 us; the launch traced here: 250 us
  waiting for transfers between devices  105 us (42%)
  matrix products  79.3 us (32%)
  other arithmetic  28.5 us (11%)
  local copies, waits for them, and re-layouts  23.2 us (9%)
  starting transfers between devices  12.2 us (5%)
    ppermute x9, waiting for transfers between devices, partner_2(): return lax.ppermute(block, axis, route)  105 us
    dot_general x8, matrix products, group_output(): jnp.einsum('gts,sgp->tgp', mixing, group_values, preferred_element_type=j...  59.6 us
    dot_general x8, matrix products, group_output(): jnp.einsum('gtk,gkp->tgp', read_rows, group_states, preferred_element_typ...  16.1 us
    eq x40, other arithmetic, group_output(): level_map[None] == level_no  13 us
    ppermute x9, starting transfers between devices, partner_2(): return lax.ppermute(block, axis, route)  12.2 us
    squeeze x8, local copies, waits for them, and re-layouts, local(): lax.map(group_output, (sum_grouped, weight_grouped, values_grouped, state...  7.99 us
    unnamed x5, local copies, waits for them, and re-layouts  6.82 us
  transfers between devices with their start and end apart: 9, of which 5 were waited for; matrix products, arithmetic and copies ran while one was open for 4% of the time, Pallas kernels for 0%

commit v1 on v0

v1 whole, which is shorter than its diff:
```python
import functools

import jax
import jax.numpy as jnp
from jax import lax
from jax.experimental import pallas as pl
from jax.experimental.pallas import tpu as pltpu
from jax.sharding import PartitionSpec as P

MESH = pl.DeviceIdType.MESH
LANES = 128
CHUNKS = 4
F32 = jnp.float32
BF16 = jnp.bfloat16


def bit_length_map(differ, bits):
    out = jnp.zeros(differ.shape, jnp.int32)
    for power in range(bits):
        out = out + (differ >= (1 << power)).astype(jnp.int32)
    return out


def split3(value):
    high = value.astype(BF16)
    rest = value - high.astype(F32)
    middle = rest.astype(BF16)
    low = (rest - middle.astype(F32)).astype(BF16)
    return high, middle, low


def lanes_at(table, index):
    return jnp.take_along_axis(table, index, axis=1, mode="promise_in_bounds")


def kernel(
    count, heads, slot,
    x_ref, kq_ref, step_ref, logit_ref, rate_ref, reset_ref, out_ref,
    scores, weight, fall, ending, whole, keys_t, query2, acc, state, current, arrived,
    send_sem, recv_sem, pass_sem,
):
    length = x_ref.shape[0]
    state_dim = kq_ref.shape[1] // 2
    bits = count.bit_length() - 1
    inner = length.bit_length()
    tiles = length // LANES
    pairs = heads // 2
    half_pairs = pairs // 2
    per_chunk = half_pairs // CHUNKS
    total_row = per_chunk * state_dim
    per_group = LANES // slot
    levels = logit_ref.shape[1] // heads

    me = lax.axis_index("seq")
    core = me % 2

    def upper(bit):
        return (me // (1 << bit)) % 2

    def partner(bit):
        return me + (1 - 2 * upper(bit)) * (1 << bit)

    barrier = pltpu.get_barrier_semaphore()
    for bit in range(bits):
        pl.semaphore_signal(barrier, inc=1, device_id=(partner(bit),), device_id_type=MESH)

    steps = -(step_ref[...] * rate_ref[...])
    spread = (
        lax.broadcasted_iota(jnp.int32, (heads, LANES), 1) % heads
        == lax.broadcasted_iota(jnp.int32, (heads, LANES), 0)
    ).astype(F32).astype(BF16)
    lower = (
        lax.broadcasted_iota(jnp.int32, (length, length), 0)
        >= lax.broadcasted_iota(jnp.int32, (length, length), 1)
    ).astype(F32).astype(BF16)
    cum = jnp.zeros((length, LANES), F32)
    for part in split3(steps):
        wide = jnp.dot(part, spread, preferred_element_type=F32).astype(BF16)
        cum = cum + jnp.dot(lower, wide, preferred_element_type=F32)
    cum_t = jnp.transpose(cum)[:heads, :]
    fall[...] = jnp.exp(-cum_t)
    last = cum_t[:, length - 1:length]
    ending[...] = jnp.exp(last - cum_t)
    whole[...] = jnp.broadcast_to(jnp.exp(last), (heads, LANES))
    lane = lax.broadcasted_iota(jnp.int32, (1, LANES), 1)
    left = lane < state_dim
    pair_rows = kq_ref[...].astype(F32)
    keys_t[...] = jnp.transpose(pair_rows)[:state_dim, :]
    entering = 1.0 - reset_ref[0].astype(F32)

    pl.semaphore_wait(barrier, bits)

    def state_copy(half, chunk):
        return pltpu.make_async_remote_copy(
            src_ref=state.at[half, chunk], dst_ref=arrived.at[0, half, chunk],
            send_sem=send_sem.at[0, half, chunk], recv_sem=recv_sem.at[0, half, chunk],
            device_id=(partner(0),), device_id_type=MESH,
        )

    def range_copy(bit, chunk):
        return pltpu.make_async_remote_copy(
            src_ref=current.at[bit - 1, chunk], dst_ref=arrived.at[bit, core, chunk],
            send_sem=send_sem.at[bit, core, chunk], recv_sem=recv_sem.at[bit, core, chunk],
            device_id=(partner(bit),), device_id_type=MESH,
        )

    def pass_copy(bit, half, chunk):
        return pltpu.make_async_remote_copy(
            src_ref=arrived.at[bit, half, chunk], dst_ref=arrived.at[bit, half, chunk],
            send_sem=pass_sem.at[bit, chunk], recv_sem=recv_sem.at[bit, half, chunk],
            device_id=(partner(0),), device_id_type=MESH,
        )

    def make_state(step_no, _):
        half, chunk = step_no % 2, step_no // 2
        state[half, chunk, pl.ds(total_row, 8), :] = jnp.zeros((8, LANES), F32)
        for item in range(per_chunk):
            pair = half * half_pairs + chunk * per_chunk + item
            columns = pl.ds(pl.multiple_of(pair * LANES, LANES), LANES)
            rows = []
            for head in range(2):
                gone = ending[pl.ds(pair * 2 + head, 1), :]
                rows.append((keys_t[...] * gone).astype(BF16))
            both = jnp.dot(jnp.concatenate(rows, 0), x_ref[:, columns], preferred_element_type=F32)
            state[half, chunk, pl.ds(item * state_dim, state_dim), :] = jnp.where(
                left, both[:state_dim], both[state_dim:]
            )
            state[half, chunk, pl.ds(total_row + item, 1), :] = entering * jnp.where(
                left, whole[pl.ds(pair * 2, 1), :], whole[pl.ds(pair * 2 + 1, 1), :]
            )
        state_copy(half, chunk).start()
        return 0

    lax.fori_loop(0, 2 * CHUNKS, make_state, 0)

    turned = pltpu.roll(pair_rows, state_dim, 1)
    query2[...] = jnp.where(left, turned, pair_rows)
    width = logit_ref.shape[1]
    source = lax.broadcasted_iota(jnp.int32, (width, heads * slot), 0)
    target = lax.broadcasted_iota(jnp.int32, (width, heads * slot), 1)
    regroup = (
        (source % heads == target // slot) & (source // heads == target % slot)
    ).astype(F32).astype(BF16)
    for tile in range(tiles):
        rows = slice(tile * LANES, (tile + 1) * LANES)
        grown = jnp.exp(cum[rows])
        grown = jnp.concatenate([grown] * pl.cdiv(width, LANES), 1)[:, :width]
        logit = logit_ref[rows, :]
        soft = jnp.maximum(logit, 0.0) + jnp.log1p(jnp.exp(-jnp.abs(logit)))
        total = None
        for part in split3(soft * grown):
            term = jnp.dot(part, regroup, preferred_element_type=F32)
            total = term if total is None else total + term
        weight[rows, :] = total
    queries = jnp.where(left, turned, 0.0).astype(BF16)
    raw = lax.dot_general(
        queries, kq_ref[...], (((1,), (1,)), ((), ())), preferred_element_type=F32
    )
    scores[...] = jnp.where(
        lax.broadcasted_iota(jnp.int32, (length, length), 0)
        >= lax.broadcasted_iota(jnp.int32, (length, length), 1), raw, 0.0
    )
    row_at = lax.broadcasted_iota(jnp.int32, (LANES, LANES), 0)
    lane_at = lax.broadcasted_iota(jnp.int32, (LANES, LANES), 1)
    tile_levels = LANES.bit_length() - 1

    def on_event(bit, chunk):
        range_recv = range_copy(bit, chunk) if bit else state_copy(core, chunk)
        range_recv.wait_recv()
        if bit:
            pass_copy(bit, core, chunk).start()
        if bit == bits - 1:
            return
        own = current.at[bit - 1, chunk] if bit else state.at[core, chunk]
        is_upper = upper(bit) == 1
        mine_total = own[pl.ds(total_row, 8), :]
        other_total = arrived[bit, core, chunk, pl.ds(total_row, 8), :]
        for item in range(per_chunk):
            span = pl.ds(item * state_dim, state_dim)
            mine, other = own[span, :], arrived[bit, core, chunk, span, :]
            early = jnp.where(is_upper, other, mine)
            late = jnp.where(is_upper, mine, other)
            late_total = jnp.where(is_upper, mine_total, other_total)[item:item + 1]
            current[bit, chunk, span, :] = late + late_total * early
        current[bit, chunk, pl.ds(total_row, 8), :] = mine_total * other_total
        range_copy(bit + 1, chunk).start()

    events = {}
    for bit in range(bits):
        for chunk in range(CHUNKS):
            due = min(pairs, max(0, 1 + (bit * 5) // 2 + (chunk * 3) // 2))
            events.setdefault(due, []).append((bit, chunk))

    def local_pair(pair, _):
        for due in range(pairs):
            if due in events:
                @pl.when(pair == due)
                def _():
                    for bit, chunk in events[due]:
                        on_event(bit, chunk)
        columns = pl.ds(pl.multiple_of(pair * LANES, LANES), LANES)
        group = pl.ds(pl.multiple_of((pair * 2 // per_group) * LANES, LANES), LANES)
        base = (pair * 2 % per_group) * slot
        for tile in range(tiles):
            rows = slice(tile * LANES, (tile + 1) * LANES)
            table = weight[rows, group]
            done = []
            for head in range(2):
                first = base + head * slot
                gain = {}
                strip = []
                drop = fall[pl.ds(pair * 2 + head, 1), :]
                for past in range(tile + 1):
                    level = tile_levels + (tile ^ past).bit_length()
                    if past == tile:
                        near = bit_length_map(row_at ^ lane_at, tile_levels)
                        gain[level] = lanes_at(table, near + first)
                    elif level not in gain:
                        gain[level] = lanes_at(table, jnp.full((LANES, LANES), level, jnp.int32) + first)
                    span = slice(past * LANES, (past + 1) * LANES)
                    strip.append((scores[rows, span] * drop[:, span] * gain[level]).astype(BF16))
                strip = jnp.concatenate(strip, 1) if tile else strip[0]
                done.append(jnp.dot(
                    strip, x_ref[:(tile + 1) * LANES, columns], preferred_element_type=F32
                ))
            acc[rows, columns] = jnp.where(left, done[0], done[1])
        return 0

    lax.fori_loop(0, pairs, local_pair, 0)
    for bit, chunk in events.get(pairs, []):
        on_event(bit, chunk)

    for chunk in range(CHUNKS):
        state_copy(1 - core, chunk).wait_recv()
        for bit in range(1, bits):
            pass_copy(bit, 1 - core, chunk).wait_recv()

    couples = pl.cdiv(bits, 2)

    def cross_pair(pair, _):
        half = pair // half_pairs
        chunk = pair % half_pairs // per_chunk
        item = pair % per_chunk
        columns = pl.ds(pl.multiple_of(pair * LANES, LANES), LANES)
        group = pl.ds(pl.multiple_of((pair * 2 // per_group) * LANES, LANES), LANES)
        base = (pair * 2 % per_group) * slot
        prefix = jnp.ones((1, LANES), F32) * entering
        stack = []
        for bit in range(bits):
            is_upper = upper(bit) == 1
            other = arrived[bit, half, chunk, pl.ds(pl.multiple_of(item * state_dim, state_dim), state_dim), :]
            other_total = arrived[bit, half, chunk, pl.ds(total_row + item, 1), :]
            stack.append((other * jnp.where(is_upper, prefix, 0.0)).astype(BF16))
            prefix = jnp.where(is_upper, prefix * other_total, prefix)
        if bits % 2:
            stack.append(jnp.zeros((state_dim, LANES), BF16))
        stack = jnp.concatenate(stack, 0)
        for tile in range(tiles):
            rows = slice(tile * LANES, (tile + 1) * LANES)
            table = weight[rows, group]
            done = []
            for head in range(2):
                reads = []
                for couple in range(couples):
                    at = jnp.where(lane_at < state_dim, 0, 1) + (base + head * slot + inner + 2 * couple)
                    reads.append((lanes_at(table, at) * query2[rows, :]).astype(BF16))
                done.append(jnp.dot(jnp.concatenate(reads, 1), stack, preferred_element_type=F32))
            out_ref[rows, columns] = (
                acc[rows, columns] + jnp.where(left, done[0], done[1])
            ).astype(BF16)
        return 0

    lax.fori_loop(0, pairs, cross_pair, 0)

    for chunk in range(CHUNKS):
        for half in range(2):
            state_copy(half, chunk).wait_send()
        for bit in range(1, bits):
            range_copy(bit, chunk).wait_send()
            pass_copy(bit, core, chunk).wait_send()


def solution(mesh):
    count = mesh.shape["seq"]
    bits = count.bit_length() - 1

    def local(values, keys_queries, step_size, level_logits, decay_rate, resets):
        length, columns = values.shape
        heads = decay_rate.shape[0]
        state_dim = keys_queries.shape[1] // 2
        levels = level_logits.shape[1] // heads
        slot = 1 << levels.bit_length()
        chunk_rows = heads // 4 // CHUNKS * state_dim + 8
        vmem = pl.BlockSpec(memory_space=pltpu.VMEM)
        return pl.pallas_call(
            functools.partial(kernel, count, heads, slot),
            out_shape=jax.ShapeDtypeStruct((length, columns), values.dtype),
            in_specs=[vmem] * 5 + [pl.BlockSpec(memory_space=pltpu.SMEM)],
            out_specs=vmem,
            scratch_shapes=[
                pltpu.VMEM((length, length), F32),
                pltpu.VMEM((length, heads * slot), F32),
                pltpu.VMEM((heads, length), F32),
                pltpu.VMEM((heads, length), F32),
                pltpu.VMEM((heads, LANES), F32),
                pltpu.VMEM((state_dim, length), F32),
                pltpu.VMEM((length, 2 * state_dim), F32),
                pltpu.VMEM((length, columns), F32),
                pltpu.VMEM((2, CHUNKS, chunk_rows, LANES), F32),
                pltpu.VMEM((bits - 1, CHUNKS, chunk_rows, LANES), F32),
                pltpu.VMEM((bits, 2, CHUNKS, chunk_rows, LANES), F32),
                pltpu.SemaphoreType.DMA((bits, 2, CHUNKS)),
                pltpu.SemaphoreType.DMA((bits, 2, CHUNKS)),
                pltpu.SemaphoreType.DMA((bits, CHUNKS)),
            ],
            compiler_params=pltpu.CompilerParams(
                collective_id=0, has_side_effects=True, vmem_limit_bytes=64000000
            ),
        )(values, keys_queries, step_size, level_logits, decay_rate.reshape(1, heads), resets)

    placed = (P("seq", None), P("seq", None), P("seq", None), P("seq", None), P(), P("seq"))
    return jax.shard_map(
        local, mesh=mesh, in_specs=placed, out_specs=P("seq", None), check_vma=False
    )
```

time: 251 us -> 60 us (0.24)
  waiting for transfers between devices: 105 us -> 0 us
  matrix products: 79.3 us -> 0 us
  Pallas kernels: 0 us -> 51.7 us
  other arithmetic: 28.5 us -> 0 us
  local copies, waits for them, and re-layouts: 23.2 us -> 7.36 us
  starting transfers between devices: 12.2 us -> 0 us
    ppermute x9 -> x0, waiting for transfers between devices: 105 us -> none  [partner_2(): return lax.ppermute(block, axis, route)]
    dot_general x18 -> x0, matrix products: 79.3 us -> none  [the longest x8 59.6 us: group_output(): jnp.einsum('gts,sgp->tgp', mixing, group_values, preferred_element_type=j...]
    pallas_call x0 -> x1, Pallas kernels: none -> 51.7 us  [local(): pl.pallas_call(functools.partial(kernel, count, heads, slot), out_shape=j...]
    eq x40 -> x0, other arithmetic: 13 us -> none  [group_output(): level_map[None] == level_no]
    ppermute x9 -> x0, starting transfers between devices: 12.2 us -> none  [partner_2(): return lax.ppermute(block, axis, route)]
    squeeze x8 -> x0, local copies, waits for them, and re-layouts: 7.99 us -> none  [local(): lax.map(group_output, (sum_grouped, weight_grouped, values_grouped, state...]
    select_n x5 -> x0, other arithmetic: 6.24 us -> none  [the longest x4 3.55 us: local(): jnp.where(in_upper, range_state + range_total[:, None, None] * partner, p...]
    convert_element_type x1 -> x0, local copies, waits for them, and re-layouts: 3.91 us -> none  [local(): outputs.transpose(1, 0, 2, 3).reshape(length, head_count * head_dim)]
  transfers between devices with their start and end apart: 9 -> 0, of which waited for: 5 -> 0; matrix products, arithmetic and copies ran while one was open for 4% -> 0% of each run, Pallas kernels for 0% -> 0%
where the time goes in v1:
time: 60 us; the launch traced here: 59.7 us
  Pallas kernels  51.7 us (86%)
  local copies, waits for them, and re-layouts  7.36 us (12%)
  between operations  0.66 us (1%)
    pallas_call x1, Pallas kernels, local(): pl.pallas_call(functools.partial(kernel, count, heads, slot), out_shape=j...  51.7 us
    unnamed x3, local copies, waits for them, and re-layouts  7.36 us

profile of v1, /device:TPU:0, one launch (start us, length us, event | category | flops | bytes accessed | tf_op | source)
XLA Modules:
  0.0 59.7 jit_solution(17613389915099553900)
XLA Ops:
  0.7 1.7 %copy.7.step_ref = f32[512,32]{1,0:T(8,128)} copy(f32[512,32]{0,1:T(8,128)} %param.8) | data formatting | bytes 131072 | tf_op args[2]
  2.4 2.5 %copy.8.logit_ref = f32[512,480]{1,0:T(8,128)} copy(f32[512,480]{0,1:T(8,128)} %param.9) | data formatting | bytes 1966080 | tf_op args[3]
  4.9 51.7 %shard_map.64 = bf16[512,2048]{1,0:T(8,128)(2,1)} custom-call(bf16[512,2048]{1,0:T(8,128)(2,1)} %x_ref.1, bf16[512,128]{1,0:T(8,128)(2,1)} %kq_ref.1, f32[512,32]{1,0:T(8,128)} %copy.7.step_ref, f32[512,480]{1,0:T(8,128)} %copy.8.logit_ref, f32[1,32]{1,0:T(1,128)} %bitcast.1, s32[1]{0:T(128)S(6)} %copy.10.reset_ref), custom_call_target="tpu_custom_call" | custom-call | tf_op jit(solution)/shard_map/pallas_call | solution.py:295
  56.6 3.2 %copy.11 = bf16[512,2048]{1,0:T(8,128)(2,1)} copy(bf16[512,2048]{1,0:T(8,128)(2,1)} %shard_map.64) | data formatting | bytes 4194304

commit v2 on v1

--- a/solution.py
+++ b/solution.py
@@ -30,14 +30,21 @@
 
 
 def lanes_at(table, index):
-    return jnp.take_along_axis(table, index, axis=1, mode="promise_in_bounds")
+    picks = lax.GatherDimensionNumbers(
+        offset_dims=(), collapsed_slice_dims=(1,), start_index_map=(1,),
+        operand_batching_dims=(0,), start_indices_batching_dims=(0,),
+    )
+    return lax.gather(
+        table, index[..., None], picks, (1, 1), mode=lax.GatherScatterMode.PROMISE_IN_BOUNDS
+    )
 
 
 def kernel(
     count, heads, slot,
-    x_ref, kq_ref, step_ref, logit_ref, rate_ref, reset_ref, out_ref,
+    x_hbm, logit_hbm, kq_ref, step_ref, rate_ref, reset_ref, out_hbm,
+    x_ref, logit_ref, out_ref, final_reads,
     scores, weight, fall, ending, whole, keys_t, query2, acc, state, current, arrived,
-    send_sem, recv_sem, pass_sem,
+    send_sem, recv_sem, pass_sem, in_sem, out_sem,
 ):
     length = x_ref.shape[0]
     state_dim = kq_ref.shape[1] // 2
@@ -49,7 +56,6 @@
     per_chunk = half_pairs // CHUNKS
     total_row = per_chunk * state_dim
     per_group = LANES // slot
-    levels = logit_ref.shape[1] // heads
 
     me = lax.axis_index("seq")
     core = me % 2
@@ -60,24 +66,22 @@
     def partner(bit):
         return me + (1 - 2 * upper(bit)) * (1 << bit)
 
+    x_load = pltpu.make_async_copy(x_hbm, x_ref, in_sem.at[0])
+    logit_load = pltpu.make_async_copy(logit_hbm, logit_ref, in_sem.at[1])
+    x_load.start()
+    logit_load.start()
     barrier = pltpu.get_barrier_semaphore()
     for bit in range(bits):
         pl.semaphore_signal(barrier, inc=1, device_id=(partner(bit),), device_id_type=MESH)
 
     steps = -(step_ref[...] * rate_ref[...])
-    spread = (
-        lax.broadcasted_iota(jnp.int32, (heads, LANES), 1) % heads
-        == lax.broadcasted_iota(jnp.int32, (heads, LANES), 0)
+    earlier = (
+        lax.broadcasted_iota(jnp.int32, (length, length), 0)
+        <= lax.broadcasted_iota(jnp.int32, (length, length), 1)
     ).astype(F32).astype(BF16)
-    lower = (
-        lax.broadcasted_iota(jnp.int32, (length, length), 0)
-        >= lax.broadcasted_iota(jnp.int32, (length, length), 1)
-    ).astype(F32).astype(BF16)
-    cum = jnp.zeros((length, LANES), F32)
-    for part in split3(steps):
-        wide = jnp.dot(part, spread, preferred_element_type=F32).astype(BF16)
-        cum = cum + jnp.dot(lower, wide, preferred_element_type=F32)
-    cum_t = jnp.transpose(cum)[:heads, :]
+    sums = jnp.dot(jnp.concatenate(split3(steps), 0), earlier, preferred_element_type=F32)
+    cum_t = sums[:heads] + sums[heads:2 * heads] + sums[2 * heads:]
+    grown = jnp.exp(cum_t)
     fall[...] = jnp.exp(-cum_t)
     last = cum_t[:, length - 1:length]
     ending[...] = jnp.exp(last - cum_t)
@@ -89,6 +93,7 @@
     entering = 1.0 - reset_ref[0].astype(F32)
 
     pl.semaphore_wait(barrier, bits)
+    x_load.wait()
 
     def state_copy(half, chunk):
         return pltpu.make_async_remote_copy(
@@ -135,7 +140,8 @@
 
     turned = pltpu.roll(pair_rows, state_dim, 1)
     query2[...] = jnp.where(left, turned, pair_rows)
-    width = logit_ref.shape[1]
+    logit_load.wait()
+    width = logit_ref.shape[0]
     source = lax.broadcasted_iota(jnp.int32, (width, heads * slot), 0)
     target = lax.broadcasted_iota(jnp.int32, (width, heads * slot), 1)
     regroup = (
@@ -143,13 +149,14 @@
     ).astype(F32).astype(BF16)
     for tile in range(tiles):
         rows = slice(tile * LANES, (tile + 1) * LANES)
-        grown = jnp.exp(cum[rows])
-        grown = jnp.concatenate([grown] * pl.cdiv(width, LANES), 1)[:, :width]
-        logit = logit_ref[rows, :]
+        logit = logit_ref[:, rows]
         soft = jnp.maximum(logit, 0.0) + jnp.log1p(jnp.exp(-jnp.abs(logit)))
+        soft = soft * jnp.concatenate([grown[:, rows]] * (width // heads), 0)
         total = None
-        for part in split3(soft * grown):
-            term = jnp.dot(part, regroup, preferred_element_type=F32)
+        for part in split3(soft):
+            term = lax.dot_general(
+                part, regroup, (((0,), (0,)), ((), ())), preferred_element_type=F32
+            )
             total = term if total is None else total + term
         weight[rows, :] = total
     queries = jnp.where(left, turned, 0.0).astype(BF16)
@@ -185,19 +192,24 @@
         current[bit, chunk, pl.ds(total_row, 8), :] = mine_total * other_total
         range_copy(bit + 1, chunk).start()
 
-    events = {}
-    for bit in range(bits):
+    events, late_events = {}, {}
+    for bit in range(bits - 1):
         for chunk in range(CHUNKS):
-            due = min(pairs, max(0, 1 + (bit * 5) // 2 + (chunk * 3) // 2))
+            due = min(pairs - 1, 1 + (bit * 5) // 2 + (chunk * 3) // 2)
             events.setdefault(due, []).append((bit, chunk))
+    for chunk in range(CHUNKS):
+        due = min(pairs - 1, 2 + chunk * pairs // CHUNKS)
+        late_events.setdefault(due, []).append((bits - 1, chunk))
+
+    def run_events(table, pair):
+        for due in table:
+            @pl.when(pair == due)
+            def _():
+                for bit, chunk in table[due]:
+                    on_event(bit, chunk)
 
     def local_pair(pair, _):
-        for due in range(pairs):
-            if due in events:
-                @pl.when(pair == due)
-                def _():
-                    for bit, chunk in events[due]:
-                        on_event(bit, chunk)
+        run_events(events, pair)
         columns = pl.ds(pl.multiple_of(pair * LANES, LANES), LANES)
         group = pl.ds(pl.multiple_of((pair * 2 // per_group) * LANES, LANES), LANES)
         base = (pair * 2 % per_group) * slot
@@ -216,7 +228,8 @@
                         near = bit_length_map(row_at ^ lane_at, tile_levels)
                         gain[level] = lanes_at(table, near + first)
                     elif level not in gain:
-                        gain[level] = lanes_at(table, jnp.full((LANES, LANES), level, jnp.int32) + first)
+                        at = jnp.full((1, LANES), level, jnp.int32) + first
+                        gain[level] = lanes_at(table, jnp.broadcast_to(at, (LANES, LANES)))
                     span = slice(past * LANES, (past + 1) * LANES)
                     strip.append((scores[rows, span] * drop[:, span] * gain[level]).astype(BF16))
                 strip = jnp.concatenate(strip, 1) if tile else strip[0]
@@ -227,51 +240,78 @@
         return 0
 
     lax.fori_loop(0, pairs, local_pair, 0)
-    for bit, chunk in events.get(pairs, []):
-        on_event(bit, chunk)
 
     for chunk in range(CHUNKS):
         state_copy(1 - core, chunk).wait_recv()
-        for bit in range(1, bits):
+        for bit in range(1, bits - 1):
             pass_copy(bit, 1 - core, chunk).wait_recv()
 
-    couples = pl.cdiv(bits, 2)
-
-    def cross_pair(pair, _):
+    def level_blocks(half, chunk, item, first, end):
+        prefix = jnp.ones((1, LANES), F32) * entering
+        blocks = []
+        for bit in range(end):
+            is_upper = upper(bit) == 1
+            if bit >= first:
+                other = arrived[bit, half, chunk, pl.ds(pl.multiple_of(item * state_dim, state_dim), state_dim), :]
+                level = other * jnp.where(is_upper, prefix, 0.0)
+                blocks.append(jnp.where(left, level, 0.0).astype(BF16))
+                blocks.append(jnp.where(left, 0.0, level).astype(BF16))
+            if bit < end - 1:
+                other_total = arrived[bit, half, chunk, pl.ds(total_row + item, 1), :]
+                prefix = jnp.where(is_upper, prefix * other_total, prefix)
+        return jnp.concatenate(blocks, 0)
+
+    def early_pair(pair, _):
+        run_events(late_events, pair)
         half = pair // half_pairs
         chunk = pair % half_pairs // per_chunk
         item = pair % per_chunk
         columns = pl.ds(pl.multiple_of(pair * LANES, LANES), LANES)
         group = pl.ds(pl.multiple_of((pair * 2 // per_group) * LANES, LANES), LANES)
         base = (pair * 2 % per_group) * slot
-        prefix = jnp.ones((1, LANES), F32) * entering
-        stack = []
-        for bit in range(bits):
-            is_upper = upper(bit) == 1
-            other = arrived[bit, half, chunk, pl.ds(pl.multiple_of(item * state_dim, state_dim), state_dim), :]
-            other_total = arrived[bit, half, chunk, pl.ds(total_row + item, 1), :]
-            stack.append((other * jnp.where(is_upper, prefix, 0.0)).astype(BF16))
-            prefix = jnp.where(is_upper, prefix * other_total, prefix)
-        if bits % 2:
-            stack.append(jnp.zeros((state_dim, LANES), BF16))
-        stack = jnp.concatenate(stack, 0)
+        stack = level_blocks(half, chunk, item, 0, bits - 1)
         for tile in range(tiles):
             rows = slice(tile * LANES, (tile + 1) * LANES)
             table = weight[rows, group]
-            done = []
-            for head in range(2):
-                reads = []
-                for couple in range(couples):
-                    at = jnp.where(lane_at < state_dim, 0, 1) + (base + head * slot + inner + 2 * couple)
-                    reads.append((lanes_at(table, at) * query2[rows, :]).astype(BF16))
-                done.append(jnp.dot(jnp.concatenate(reads, 1), stack, preferred_element_type=F32))
-            out_ref[rows, columns] = (
-                acc[rows, columns] + jnp.where(left, done[0], done[1])
+            reads = []
+            for bit in range(bits):
+                at = jnp.where(left, 0, slot) + (base + inner + bit)
+                gain = lanes_at(table, jnp.broadcast_to(at, (LANES, LANES)))
+                reads.append((gain * query2[rows, :]).astype(BF16))
+            final_reads[rows, columns] = reads.pop()
+            acc[rows, columns] += jnp.dot(
+                jnp.concatenate(reads, 1), stack, preferred_element_type=F32
+            )
+        return 0
+
+    lax.fori_loop(0, pairs, early_pair, 0)
+
+    def out_copy(pair):
+        columns = pl.ds(pl.multiple_of(pair * LANES, LANES), LANES)
+        return pltpu.make_async_copy(
+            out_ref.at[:, columns], out_hbm.at[:, columns], out_sem.at[pair]
+        )
+
+    def final_chunk(chunk, _):
+        pass_copy(bits - 1, 1 - core, chunk).wait_recv()
+
+        def final_pair(number, _):
+            half, item = number // per_chunk, number % per_chunk
+            pair = half * half_pairs + chunk * per_chunk + item
+            columns = pl.ds(pl.multiple_of(pair * LANES, LANES), LANES)
+            stack = level_blocks(half, chunk, item, bits - 1, bits)
+            out_ref[:, columns] = (
+                acc[:, columns]
+                + jnp.dot(final_reads[:, columns], stack, preferred_element_type=F32)
             ).astype(BF16)
-        return 0
-
-    lax.fori_loop(0, pairs, cross_pair, 0)
-
+            out_copy(pair).start()
+            return 0
+
+        return lax.fori_loop(0, 2 * per_chunk, final_pair, 0)
+
+    lax.fori_loop(0, CHUNKS, final_chunk, 0)
+
+    lax.fori_loop(0, pairs, lambda pair, _: (out_copy(pair).wait(), 0)[1], 0)
     for chunk in range(CHUNKS):
         for half in range(2):
             state_copy(half, chunk).wait_send()
@@ -292,12 +332,17 @@
         slot = 1 << levels.bit_length()
         chunk_rows = heads // 4 // CHUNKS * state_dim + 8
         vmem = pl.BlockSpec(memory_space=pltpu.VMEM)
+        any_space = pl.BlockSpec(memory_space=pl.ANY)
         return pl.pallas_call(
             functools.partial(kernel, count, heads, slot),
             out_shape=jax.ShapeDtypeStruct((length, columns), values.dtype),
-            in_specs=[vmem] * 5 + [pl.BlockSpec(memory_space=pltpu.SMEM)],
-            out_specs=vmem,
+            in_specs=[any_space] * 2 + [vmem] * 3 + [pl.BlockSpec(memory_space=pltpu.SMEM)],
+            out_specs=any_space,
             scratch_shapes=[
+                pltpu.VMEM((length, columns), BF16),
+                pltpu.VMEM((levels * heads, length), F32),
+                pltpu.VMEM((length, columns), BF16),
+                pltpu.VMEM((length, columns), BF16),
                 pltpu.VMEM((length, length), F32),
                 pltpu.VMEM((length, heads * slot), F32),
                 pltpu.VMEM((heads, length), F32),
@@ -312,11 +357,13 @@
                 pltpu.SemaphoreType.DMA((bits, 2, CHUNKS)),
                 pltpu.SemaphoreType.DMA((bits, 2, CHUNKS)),
                 pltpu.SemaphoreType.DMA((bits, CHUNKS)),
+                pltpu.SemaphoreType.DMA((2,)),
+                pltpu.SemaphoreType.DMA((heads // 2,)),
             ],
             compiler_params=pltpu.CompilerParams(
                 collective_id=0, has_side_effects=True, vmem_limit_bytes=64000000
             ),
-        )(values, keys_queries, step_size, level_logits, decay_rate.reshape(1, heads), resets)
+        )(values, level_logits.T, keys_queries, step_size.T, decay_rate.reshape(heads, 1), resets)
 
     placed = (P("seq", None), P("seq", None), P("seq", None), P("seq", None), P(), P("seq"))
     return jax.shard_map(

time: 60 us -> 53 us (0.88)
  Pallas kernels: 51.7 us -> 47.7 us
  local copies, waits for them, and re-layouts: 7.36 us -> 4.5 us
    unnamed x3 -> x1, local copies, waits for them, and re-layouts: 7.36 us -> 3.16 us
    pallas_call x1, Pallas kernels: 51.7 us -> 47.7 us  [local(): pl.pallas_call(functools.partial(kernel, count, heads, slot), out_shape=j...]
    reshape x0 -> x1, local copies, waits for them, and re-layouts: none -> 1.34 us  [local(): decay_rate.reshape(heads, 1)]
where the time goes in v2:
time: 53 us; the launch traced here: 52.9 us
  Pallas kernels  47.7 us (90%)
  local copies, waits for them, and re-layouts  4.5 us (8%)
  between operations  0.66 us (1%)
    pallas_call x1, Pallas kernels, local(): pl.pallas_call(functools.partial(kernel, count, heads, slot), out_shape=j...  47.7 us
    unnamed x1, local copies, waits for them, and re-layouts  3.16 us
    reshape x1, local copies, waits for them, and re-layouts, local(): decay_rate.reshape(heads, 1)  1.34 us

profile of v2, /device:TPU:0, one launch (start us, length us, event | category | flops | bytes accessed | tf_op | source)
XLA Modules:
  0.0 52.9 jit_solution(13182288363237772062)
XLA Ops:
  0.7 1.3 %copy.7.rate_ref = f32[32,1]{1,0:T(8,128)} copy(f32[32,1]{0,1:T(1,128)} %bitcast.5) | data formatting | bytes 256 | tf_op jit(solution)/shard_map/reshape | solution.py:366
  2.0 47.7 %shard_map.64 = bf16[512,2048]{1,0:T(8,128)(2,1)} custom-call(bf16[512,2048]{1,0:T(8,128)(2,1)} %x_hbm.1, f32[480,512]{1,0:T(8,128)} %bitcast.3, bf16[512,128]{1,0:T(8,128)(2,1)} %kq_ref.1, f32[32,512]{1,0:T(8,128)} %bitcast.4, f32[32,1]{1,0:T(8,128)} %copy.7.rate_ref, s32[1]{0:T(128)S(6)} %copy.9.reset_ref), custom_call_target="tpu_custom_call" | custom-call | tf_op jit(solution)/shard_map/pallas_call | solution.py:336
  49.7 3.2 %copy.10 = bf16[512,2048]{1,0:T(8,128)(2,1)} copy(bf16[512,2048]{1,0:T(8,128)(2,1)} %shard_map.64) | data formatting | bytes 4194304

commit v3 on v2

--- a/solution.py
+++ b/solution.py
@@ -9,6 +9,9 @@
 
 MESH = pl.DeviceIdType.MESH
 LANES = 128
+SCALE = 1.5
+PREP = 5.0
+LATE = 4
 CHUNKS = 4
 F32 = jnp.float32
 BF16 = jnp.bfloat16
@@ -74,7 +77,12 @@
     for bit in range(bits):
         pl.semaphore_signal(barrier, inc=1, device_id=(partner(bit),), device_id_type=MESH)
 
-    steps = -(step_ref[...] * rate_ref[...])
+    diagonal = (
+        lax.broadcasted_iota(jnp.int32, (heads, heads), 0)
+        == lax.broadcasted_iota(jnp.int32, (heads, heads), 1)
+    )
+    rates = jnp.sum(jnp.where(diagonal, rate_ref[...], 0.0), axis=1, keepdims=True)
+    steps = -(step_ref[...] * rates)
     earlier = (
         lax.broadcasted_iota(jnp.int32, (length, length), 0)
         <= lax.broadcasted_iota(jnp.int32, (length, length), 1)
@@ -137,6 +145,42 @@
         return 0
 
     lax.fori_loop(0, 2 * CHUNKS, make_state, 0)
+
+    prep_events, events, late_events = {}, {}, {}
+    for bit in range(1, bits - 1):
+        for chunk in range(CHUNKS):
+            due = SCALE * (3.0 + 3.2 * (bit - 1) + 1.5 * chunk)
+            if due < PREP:
+                prep_events.setdefault(int(due * tiles / PREP), []).append((bit, chunk))
+            else:
+                due = min(pairs - 1, int((due - PREP) / 0.8))
+                events.setdefault(due, []).append((bit, chunk))
+    for chunk in range(CHUNKS):
+        due = min(pairs - 1, LATE + chunk * pairs // (CHUNKS + 1))
+        late_events.setdefault(due, []).append((bits - 1, chunk))
+    def on_event(bit, chunk):
+        range_recv = range_copy(bit, chunk) if bit else state_copy(core, chunk)
+        range_recv.wait_recv()
+        if bit:
+            pass_copy(bit, core, chunk).start()
+        if bit == bits - 1:
+            return
+        own = current.at[bit - 1, chunk] if bit else state.at[core, chunk]
+        is_upper = upper(bit) == 1
+        mine_total = own[pl.ds(total_row, 8), :]
+        other_total = arrived[bit, core, chunk, pl.ds(total_row, 8), :]
+        for item in range(per_chunk):
+            span = pl.ds(item * state_dim, state_dim)
+            mine, other = own[span, :], arrived[bit, core, chunk, span, :]
+            early = jnp.where(is_upper, other, mine)
+            late = jnp.where(is_upper, mine, other)
+            late_total = jnp.where(is_upper, mine_total, other_total)[item:item + 1]
+            current[bit, chunk, span, :] = late + late_total * early
+        current[bit, chunk, pl.ds(total_row, 8), :] = mine_total * other_total
+        range_copy(bit + 1, chunk).start()
+
+    for chunk in range(CHUNKS):
+        on_event(0, chunk)
 
     turned = pltpu.roll(pair_rows, state_dim, 1)
     query2[...] = jnp.where(left, turned, pair_rows)
@@ -159,6 +203,8 @@
             )
             total = term if total is None else total + term
         weight[rows, :] = total
+        for bit, chunk in prep_events.get(tile, []):
+            on_event(bit, chunk)
     queries = jnp.where(left, turned, 0.0).astype(BF16)
     raw = lax.dot_general(
         queries, kq_ref[...], (((1,), (1,)), ((), ())), preferred_element_type=F32
@@ -170,36 +216,6 @@
     row_at = lax.broadcasted_iota(jnp.int32, (LANES, LANES), 0)
     lane_at = lax.broadcasted_iota(jnp.int32, (LANES, LANES), 1)
     tile_levels = LANES.bit_length() - 1
-
-    def on_event(bit, chunk):
-        range_recv = range_copy(bit, chunk) if bit else state_copy(core, chunk)
-        range_recv.wait_recv()
-        if bit:
-            pass_copy(bit, core, chunk).start()
-        if bit == bits - 1:
-            return
-        own = current.at[bit - 1, chunk] if bit else state.at[core, chunk]
-        is_upper = upper(bit) == 1
-        mine_total = own[pl.ds(total_row, 8), :]
-        other_total = arrived[bit, core, chunk, pl.ds(total_row, 8), :]
-        for item in range(per_chunk):
-            span = pl.ds(item * state_dim, state_dim)
-            mine, other = own[span, :], arrived[bit, core, chunk, span, :]
-            early = jnp.where(is_upper, other, mine)
-            late = jnp.where(is_upper, mine, other)
-            late_total = jnp.where(is_upper, mine_total, other_total)[item:item + 1]
-            current[bit, chunk, span, :] = late + late_total * early
-        current[bit, chunk, pl.ds(total_row, 8), :] = mine_total * other_total
-        range_copy(bit + 1, chunk).start()
-
-    events, late_events = {}, {}
-    for bit in range(bits - 1):
-        for chunk in range(CHUNKS):
-            due = min(pairs - 1, 1 + (bit * 5) // 2 + (chunk * 3) // 2)
-            events.setdefault(due, []).append((bit, chunk))
-    for chunk in range(CHUNKS):
-        due = min(pairs - 1, 2 + chunk * pairs // CHUNKS)
-        late_events.setdefault(due, []).append((bits - 1, chunk))
 
     def run_events(table, pair):
         for due in table:
@@ -363,7 +379,7 @@
             compiler_params=pltpu.CompilerParams(
                 collective_id=0, has_side_effects=True, vmem_limit_bytes=64000000
             ),
-        )(values, level_logits.T, keys_queries, step_size.T, decay_rate.reshape(heads, 1), resets)
+        )(values, level_logits.T, keys_queries, step_size.T, decay_rate.reshape(1, heads), resets)
 
     placed = (P("seq", None), P("seq", None), P("seq", None), P("seq", None), P(), P("seq"))
     return jax.shard_map(

time: 53 us -> 48.1 us (0.908)
  Pallas kernels: 47.7 us -> 44.1 us
  local copies, waits for them, and re-layouts: 4.5 us -> 3.16 us
    pallas_call x1, Pallas kernels: 47.7 us -> 44.1 us  [local(): pl.pallas_call(functools.partial(kernel, count, heads, slot), out_shape=j...]
    reshape x1 -> x0, local copies, waits for them, and re-layouts: 1.34 us -> none  [local(): decay_rate.reshape(heads, 1)]
where the time goes in v3:
time: 48.1 us; the launch traced here: 47.9 us
  Pallas kernels  44.1 us (92%)
  local copies, waits for them, and re-layouts  3.16 us (7%)
  between operations  0.66 us (1%)
    pallas_call x1, Pallas kernels, local(): pl.pallas_call(functools.partial(kernel, count, heads, slot), out_shape=j...  44.1 us
    unnamed x1, local copies, waits for them, and re-layouts  3.16 us

profile of v3, /device:TPU:0, one launch (start us, length us, event | category | flops | bytes accessed | tf_op | source)
XLA Modules:
  0.0 47.9 jit_solution(2857398984726014905)
XLA Ops:
  0.7 44.1 %shard_map.64 = bf16[512,2048]{1,0:T(8,128)(2,1)} custom-call(bf16[512,2048]{1,0:T(8,128)(2,1)} %x_hbm.1, f32[480,512]{1,0:T(8,128)} %bitcast.3, bf16[512,128]{1,0:T(8,128)(2,1)} %kq_ref.1, f32[32,512]{1,0:T(8,128)} %bitcast.4, f32[1,32]{1,0:T(1,128)} %bitcast.5, s32[1]{0:T(128)S(6)} %copy.8.reset_ref), custom_call_target="tpu_custom_call" | custom-call | tf_op jit(solution)/shard_map/pallas_call | solution.py:352
  44.7 3.2 %copy.9 = bf16[512,2048]{1,0:T(8,128)(2,1)} copy(bf16[512,2048]{1,0:T(8,128)(2,1)} %shard_map.64) | data formatting | bytes 4194304
